TPU v7x, 32 devices: a whole 2x2x4 slice. The times are simulated.
32 devices in a mesh: rows: 8 (over z, core), aux: 4 (over y, x).
Axes of the slice: x: 2, y: 2, z: 4, core: 2. Of those that a mesh axis runs over, the one named last changes fastest.
Arguments:
- pair_coeffs: float32 [36000, 8192], P('aux', 'rows'), may hold values from -0.0625 to 0.0625
- pair_gaps: float32 [8192], P('rows'), may hold values from 0.2 to 20
- trial_vectors: float32 [36000, 128], P('aux'), may hold values from -0.03125 to 0.03125
Outputs:
- vectors_out: float32 [36000, 128], P('aux')
- rayleigh: float32 [128, 128], replicated
All inputs are finite; a program needn't handle non-finite values.
Results may differ from a plain program's by a relative error of at most 0.00011.
Values sent between devices are 32-bit elements; how exact they have to be, the bound alone decides.
A program may use at most 128 MiB of HBM per device.

v0:
```python
import jax
import jax.numpy as jnp
from jax import lax
from jax.sharding import PartitionSpec as P

ITERS = 2


def project(coeffs, vectors_now):
    return lax.dot_general(
        coeffs,
        vectors_now,
        (((0,), (0,)), ((), ())),
        precision=lax.Precision.HIGHEST,
        preferred_element_type=jnp.float32,
    )


def shards(pair_coeffs, pair_gaps, trial_vectors):
    highest = lax.Precision.HIGHEST
    weights = 4.0 * pair_gaps / (pair_gaps * pair_gaps + 1.0)

    def forward(vectors_now):
        projected = lax.psum(project(pair_coeffs, vectors_now), "aux")
        return (projected, weights)

    vectors_now = trial_vectors
    for step in range(ITERS):
        apply_projected, apply_row_weights = forward(vectors_now)
        scaled = apply_row_weights[:, None] * apply_projected
        partial_sum = jnp.dot(
            pair_coeffs, scaled, precision=highest, preferred_element_type=jnp.float32
        )
        applied = lax.psum(partial_sum, "rows")
        local_gram = jnp.dot(
            applied.T, applied, precision=highest, preferred_element_type=jnp.float32
        )
        correlation = lax.psum(local_gram, "aux")
        factor = jnp.linalg.cholesky(correlation)
        vectors_now = jax.scipy.linalg.solve_triangular(factor, applied.T, lower=True).T
    final_proj, row_weights = forward(vectors_now)
    local_rayleigh = jnp.dot(
        final_proj.T,
        row_weights[:, None] * final_proj,
        precision=highest,
        preferred_element_type=jnp.float32,
    )
    rayleigh = lax.psum(local_rayleigh, "rows")
    return (vectors_now, rayleigh)


def solution(mesh):
    in_specs = (P("aux", "rows"), P("rows"), P("aux", None))
    out_specs = (P("aux", None), P())
    return jax.shard_map(shards, mesh=mesh, in_specs=in_specs, out_specs=out_specs, check_vma=False)
```

profile of v0, /device:TPU:0, one launch (start us, length us, event | category | flops | bytes accessed | tf_op | source)
XLA Modules:
  0.0 741.6 jit_solution(11998312503589431034)
XLA Ops:
  7.2 0.0 all-reduce.9.cloned.1.call-start
  7.2 27.7 %fusion.19 = f32[1024,128]{0,1:T(8,128)} fusion(f32[9000,1024]{1,0:T(8,128)} %param.6, f32[9000,128]{1,0:T(8,128)} %param.8), kind=kOutput, calls=%fused_computation.33 | convolution fusion | flops 14155776000 | bytes 41996288 | tf_op jit(solution)/shard_map/dot_general | solution.py:10
  34.9 0.0 all-reduce.9.cloned.1.call-update
  34.9 0.0 all-reduce.11.cloned.1.call-start
  35.0 48.2 %all-reduce.9.cloned.1.call-done = f32[1024,128]{0,1:T(8,128)} async-done(((f32[1024,128]{0,1:T(8,128)}), f32[1024,128]{0,1:T(8,128)}) %all-reduce.9.cloned.1.call-update) | async-done | bytes 524304 | tf_op jit(solution)/shard_map/psum | solution.py:24
  83.2 33.3 %convolution_bitcast_fusion.1 = f32[9000,128]{1,0:T(8,128)} fusion(f32[9000,1024]{1,0:T(8,128)} %param.6, f32[1024,128]{0,1:T(8,128)} %all-reduce.9.cloned.1.call-done, f32[1024]{0:T(1024)S(1)} %add_divide_fusion), kind=kOutput, calls=%fused_computation.1 | convolution fusion | flops 14155907072 | bytes 42000384 | tf_op jit(solution)/shard_map/dot_general | solution.py:31
  116.5 0.0 all-reduce.11.cloned.1.call-update
  116.5 0.3 all-reduce.13.cloned.1.call-start
  116.8 104.8 %all-reduce.11.cloned.1.call-done = f32[9000,128]{1,0:T(8,128)} async-done(((f32[9000,128]{1,0:T(8,128)}), f32[9000,128]{1,0:T(8,128)}) %all-reduce.11.cloned.1.call-update) | async-done | bytes 4608016 | tf_op jit(solution)/shard_map/psum | solution.py:34
  221.5 11.8 %fusion.20 = f32[128,128]{0,1:T(8,128)} fusion(f32[9000,128]{1,0:T(8,128)} %all-reduce.11.cloned.1.call-done), kind=kOutput, calls=%fused_computation.34 | convolution fusion | flops 1769472000 | bytes 4673536 | tf_op jit(solution)/shard_map/dot_general | solution.py:35
  233.3 0.0 all-reduce.13.cloned.1.call-update
  233.3 0.4 all-reduce.15.cloned.1.call-start
  233.8 41.4 %all-reduce.13.cloned.1.call-done = f32[128,128]{0,1:T(8,128)} async-done(((f32[128,128]{0,1:T(8,128)}), f32[128,128]{0,1:T(8,128)}) %all-reduce.13.cloned.1.call-update) | async-done | bytes 65552 | tf_op jit(solution)/shard_map/psum | solution.py:38
  275.1 0.9 copy.6
  276.1 0.9 fusion.16
  276.9 11.7 %cholesky.44 = f32[128,128]{1,0:T(8,128)S(1)} custom-call(f32[128,128]{1,0:T(8,128)S(1)} %fusion.16), custom_call_target="Cholesky" | custom-call | tf_op jit(solution)/shard_map/jit(cholesky)/cholesky | solution.py:39
  288.7 0.6 compare_reduce_fusion.1
  289.3 0.7 fusion.11
  290.0 9.8 %custom-call.6 = f32[1,128,128]{1,2,0:T(8,128)S(1)} custom-call(f32[1,128,128]{2,1,0:T(8,128)S(1)} %fusion.11), custom_call_target="InvertDiagBlocksLowerTriangular" | custom-call | tf_op jit(solution)/shard_map/jit(_solve_triangular)/triangular_solve | solution.py:40
  299.8 6.1 fusion.2
  305.9 24.9 %convolution_bitcast_fusion.2 = f32[1024,128]{0,1:T(8,128)} fusion(f32[128,9000]{1,0:T(8,128)S(1)} %fusion.2, f32[9000,1024]{1,0:T(8,128)} %param.6), kind=kOutput, calls=%fused_computation.6 | convolution fusion | flops 14155776000 | bytes 41996288 | tf_op jit(solution)/shard_map/dot_general | solution.py:10
  330.8 0.0 all-reduce.15.cloned.1.call-update
  330.8 0.2 all-reduce.17.cloned.1.call-start
  331.1 45.3 %all-reduce.15.cloned.1.call-done = f32[1024,128]{0,1:T(8,128)} async-done(((f32[1024,128]{0,1:T(8,128)}), f32[1024,128]{0,1:T(8,128)}) %all-reduce.15.cloned.1.call-update) | async-done | bytes 524304 | tf_op jit(solution)/shard_map/psum | solution.py:24
  376.4 33.3 %convolution_bitcast_fusion = f32[9000,128]{1,0:T(8,128)} fusion(f32[9000,1024]{1,0:T(8,128)} %param.6, f32[1024,128]{0,1:T(8,128)} %all-reduce.15.cloned.1.call-done, f32[1024]{0:T(1024)S(1)} %add_divide_fusion), kind=kOutput, calls=%fused_computation | convolution fusion | flops 14155907072 | bytes 42000384 | tf_op jit(solution)/shard_map/dot_general | solution.py:31
  409.6 0.0 all-reduce.17.cloned.1.call-update
  409.7 0.0 all-reduce.19.cloned.1.call-start
  409.7 105.0 %all-reduce.17.cloned.1.call-done = f32[9000,128]{1,0:T(8,128)} async-done(((f32[9000,128]{1,0:T(8,128)}), f32[9000,128]{1,0:T(8,128)}) %all-reduce.17.cloned.1.call-update) | async-done | bytes 4608016 | tf_op jit(solution)/shard_map/psum | solution.py:34
  514.7 11.8 %fusion.21 = f32[128,128]{0,1:T(8,128)} fusion(f32[9000,128]{1,0:T(8,128)} %all-reduce.17.cloned.1.call-done), kind=kOutput, calls=%fused_computation.35 | convolution fusion | flops 1769472000 | bytes 4673536 | tf_op jit(solution)/shard_map/dot_general | solution.py:35
  526.5 0.0 all-reduce.19.cloned.1.call-update
  526.5 0.3 all-reduce.21.cloned.1.call-start
  526.7 41.5 %all-reduce.19.cloned.1.call-done = f32[128,128]{0,1:T(8,128)} async-done(((f32[128,128]{0,1:T(8,128)}), f32[128,128]{0,1:T(8,128)}) %all-reduce.19.cloned.1.call-update) | async-done | bytes 65552 | tf_op jit(solution)/shard_map/psum | solution.py:38
  568.3 0.9 copy.8
  569.2 0.9 fusion.14
  570.1 11.7 %cholesky.55 = f32[128,128]{1,0:T(8,128)S(1)} custom-call(f32[128,128]{1,0:T(8,128)S(1)} %fusion.14), custom_call_target="Cholesky" | custom-call | tf_op jit(solution)/shard_map/jit(cholesky)/cholesky | solution.py:39
  581.8 0.6 compare_reduce_fusion
  582.5 0.7 fusion.12
  583.1 9.8 %custom-call.7 = f32[1,128,128]{1,2,0:T(8,128)S(1)} custom-call(f32[1,128,128]{2,1,0:T(8,128)S(1)} %fusion.12), custom_call_target="InvertDiagBlocksLowerTriangular" | custom-call | tf_op jit(solution)/shard_map/jit(_solve_triangular)/triangular_solve | solution.py:40
  593.0 9.2 %fusion = f32[128,9000]{0,1:T(8,128)S(1)} fusion(f32[9000,128]{1,0:T(8,128)} %all-reduce.17.cloned.1.call-done, f32[1,128,128]{1,2,0:T(8,128)S(1)} %custom-call.7), kind=kOutput, calls=%fused_computation.2 | convolution fusion | flops 1769472000 | bytes 9281536 | tf_op jit(solution)/shard_map/jit(_solve_triangular)/triangular_solve | solution.py:40
  602.2 2.1 copy-done
  604.3 25.4 %convolution_bitcast_fusion.3 = f32[1024,128]{0,1:T(8,128)} fusion(f32[128,9000]{0,1:T(8,128)S(1)} %fusion, f32[9000,1024]{1,0:T(8,128)} %param.6), kind=kOutput, calls=%fused_computation.7 | convolution fusion | flops 14155776000 | bytes 41996288 | tf_op jit(solution)/shard_map/dot_general | solution.py:10
  629.7 0.0 all-reduce.21.cloned.1.call-update
  629.8 0.0 all-reduce.23.cloned.1.call-start
  629.8 45.5 %all-reduce.21.cloned.1.call-done = f32[1024,128]{0,1:T(8,128)} async-done(((f32[1024,128]{0,1:T(8,128)}), f32[1024,128]{0,1:T(8,128)}) %all-reduce.21.cloned.1.call-update) | async-done | bytes 524304 | tf_op jit(solution)/shard_map/psum | solution.py:24
  675.3 2.4 fusion.4
  677.7 0.0 all-reduce.23.cloned.1.call-update
  677.7 55.2 %all-reduce.23.cloned.1.call-done = f32[128,128]{1,0:T(8,128)} async-done(((f32[128,128]{1,0:T(8,128)}), f32[128,128]{1,0:T(8,128)}) %all-reduce.23.cloned.1.call-update) | async-done | bytes 65552 | tf_op jit(solution)/shard_map/psum | solution.py:48
  732.9 1.5 copy.19
  (6 shorter events, 0.1 us)
Async XLA Ops:
  7.2 27.8 %copy-start.1 = (f32[1024]{0:T(1024)S(1)}, f32[1024]{0:T(1024)}, u32[]{:S(2)}) copy-start(f32[1024]{0:T(1024)} %param.7) | copy-start | bytes 12292
  7.2 76.0 %all-reduce.9.cloned.1.call-start = ((), (), s32[]{:S(2)}) async-start(), calls=%async_computation | async-start | bytes 1048576 | tf_op jit(solution)/shard_map/psum | solution.py:24
  34.9 186.6 %all-reduce.11.cloned.1.call-start = ((), (), s32[]{:S(2)}) async-start(), calls=%async_computation.1 | async-start | bytes 9216000 | tf_op jit(solution)/shard_map/psum | solution.py:34
  116.5 158.6 %all-reduce.13.cloned.1.call-start = ((), (), s32[]{:S(2)}) async-start(), calls=%async_computation.2 | async-start | bytes 131072 | tf_op jit(solution)/shard_map/psum | solution.py:38
  233.3 143.0 %all-reduce.15.cloned.1.call-start = ((), (), s32[]{:S(2)}) async-start(), calls=%async_computation.3 | async-start | bytes 1048576 | tf_op jit(solution)/shard_map/psum | solution.py:24
  330.8 183.9 %all-reduce.17.cloned.1.call-start = ((), (), s32[]{:S(2)}) async-start(), calls=%async_computation.4 | async-start | bytes 9216000 | tf_op jit(solution)/shard_map/psum | solution.py:34
  409.7 158.6 %all-reduce.19.cloned.1.call-start = ((), (), s32[]{:S(2)}) async-start(), calls=%async_computation.5 | async-start | bytes 131072 | tf_op jit(solution)/shard_map/psum | solution.py:38
  526.5 148.8 %all-reduce.21.cloned.1.call-start = ((), (), s32[]{:S(2)}) async-start(), calls=%async_computation.6 | async-start | bytes 1048576 | tf_op jit(solution)/shard_map/psum | solution.py:24
  602.2 2.2 copy-start
  629.8 103.1 %all-reduce.23.cloned.1.call-start = ((), (), s32[]{:S(2)}) async-start(), calls=%async_computation.7 | async-start | bytes 131072 | tf_op jit(solution)/shard_map/psum | solution.py:48
Sparse Core Ops, SparseCore 0:
  35.1 48.0 all-reduce.8
  116.6 104.8 all-reduce.10
  233.5 41.6 all-reduce.12
  331.0 45.3 all-reduce.14
  409.8 104.8 all-reduce.16
  526.6 41.6 all-reduce.18
  629.9 45.3 all-reduce.20
  678.2 54.6 all-reduce.22
where the time goes:
time: 748 us; the launch traced here: 742 us
  waiting for transfers between devices  487 us (65%)
  matrix products  186 us (25%)
  other arithmetic  47.4 us (6%)
  between operations  14.6 us (2%)
    psum x2, waiting for transfers between devices, shards(): applied = lax.psum(partial_sum, 'rows')  210 us
    psum x3, waiting for transfers between devices, forward(): projected = lax.psum(project(pair_coeffs, vectors_now), 'aux')  139 us
    psum x2, waiting for transfers between devices, shards(): correlation = lax.psum(local_gram, 'aux')  82.9 us
    dot_general x3, matrix products, project(): lax.dot_general(coeffs, vectors_now, (((0,), (0,)), ((), ())), precision=...  78 us
    dot_general x2, matrix products, shards(): jnp.dot(pair_coeffs, scaled, precision=highest, preferred_element_type=jn...  66.6 us
    psum x1, waiting for transfers between devices, shards(): rayleigh = lax.psum(local_rayleigh, 'rows')  55.2 us
    another operation x6, other arithmetic, shards(): factor = jnp.linalg.cholesky(correlation)  24.8 us
    dot_general x2, matrix products, shards(): jnp.dot(applied.T, applied, precision=highest, preferred_element_type=jnp...  23.5 us
  transfers between devices with their start and end apart: 8, of which 8 were waited for; matrix products, arithmetic and copies ran while one was open for 0% of the time, Pallas kernels for 0%

commit v1 on v0

--- a/solution.py
+++ b/solution.py
@@ -31,7 +31,11 @@
         partial_sum = jnp.dot(
             pair_coeffs, scaled, precision=highest, preferred_element_type=jnp.float32
         )
-        applied = lax.psum(partial_sum, "rows")
+        size = lax.axis_size("rows")
+        applied, far = (partial_sum, 1)
+        while far < size:
+            applied = applied + lax.ppermute(applied, "rows", [(i, i ^ far) for i in range(size)])
+            far = 2 * far
         local_gram = jnp.dot(
             applied.T, applied, precision=highest, preferred_element_type=jnp.float32
         )

time: 748 us -> 1160 us (1.55)
  waiting for transfers between devices: 487 us -> 888 us
    ppermute x0 -> x6, waiting for transfers between devices: none -> 611 us  [shards(): lax.ppermute(applied, 'rows', [(i, i ^ far) for i in range(size)])]
    psum x2 -> x0, waiting for transfers between devices: 210 us -> none  [shards(): applied = lax.psum(partial_sum, 'rows')]
  transfers between devices with their start and end apart: 8 -> 12, of which waited for: 8 -> 12; matrix products, arithmetic and copies ran while one was open for 0% -> 0% of each run, Pallas kernels for 0% -> 0%
where the time goes in v1:
time: 1160 us
  waiting for transfers between devices  888 us (77%)
  matrix products  184 us (16%)
  other arithmetic  50.2 us (4%)
  between operations  14.8 us (1%)
    ppermute x6, waiting for transfers between devices, shards(): lax.ppermute(applied, 'rows', [(i, i ^ far) for i in range(size)])  611 us
    psum x3, waiting for transfers between devices, forward(): projected = lax.psum(project(pair_coeffs, vectors_now), 'aux')  139 us
    psum x2, waiting for transfers between devices, shards(): correlation = lax.psum(local_gram, 'aux')  83.2 us
    dot_general x3, matrix products, project(): lax.dot_general(coeffs, vectors_now, (((0,), (0,)), ((), ())), precision=...  78 us
    dot_general x2, matrix products, shards(): jnp.dot(pair_coeffs, scaled, precision=highest, preferred_element_type=jn...  68.9 us
    psum x1, waiting for transfers between devices, shards(): rayleigh = lax.psum(local_rayleigh, 'rows')  55 us
    another operation x6, other arithmetic, shards(): factor = jnp.linalg.cholesky(correlation)  24.8 us
  transfers between devices with their start and end apart: 12, of which 12 were waited for; matrix products, arithmetic and copies ran while one was open for 0% of the time, Pallas kernels for 0%

profile of v1, /device:TPU:0, one launch (start us, length us, event | category | flops | bytes accessed | tf_op | source)
XLA Modules:
  0.0 1156.1 jit_solution(14519239360382614564)
XLA Ops:
  7.2 27.7 %fusion.25 = f32[1024,128]{0,1:T(8,128)} fusion(f32[9000,1024]{1,0:T(8,128)} %param.6, f32[9000,128]{1,0:T(8,128)} %param.8), kind=kOutput, calls=%fused_computation.39 | convolution fusion | flops 14155776000 | bytes 41996288 | tf_op jit(solution)/shard_map/dot_general | solution.py:10
  35.0 48.2 %all-reduce.7.cloned.1.call-done = f32[1024,128]{0,1:T(8,128)} async-done(((f32[1024,128]{0,1:T(8,128)}), f32[1024,128]{0,1:T(8,128)}) %all-reduce.7.cloned.1.call-update) | async-done | bytes 524304 | tf_op jit(solution)/shard_map/psum | solution.py:24
  83.2 34.4 %convolution_bitcast_fusion.1 = f32[9000,128]{1,0:T(8,128)S(1)} fusion(f32[9000,1024]{1,0:T(8,128)} %param.6, f32[1024,128]{0,1:T(8,128)} %all-reduce.7.cloned.1.call-done, f32[1024]{0:T(1024)S(1)} %add_divide_fusion), kind=kOutput, calls=%fused_computation.1 | convolution fusion | flops 14155907072 | bytes 42000384 | tf_op jit(solution)/shard_map/dot_general | solution.py:31
  117.7 7.7 collective-permute-done
  125.5 0.5 add.47
  126.0 1.6 collective-permute-start.1
  127.5 100.0 %collective-permute-done.1 = f32[9000,128]{1,0:T(8,128)S(1)} collective-permute-done((f32[9000,128]{1,0:T(8,128)S(1)}, f32[9000,128]{1,0:T(8,128)S(1)}, u32[]{:S(2)}, u32[]{:S(2)}) %collective-permute-start.1) | collective-permute-done | bytes 4608032 | tf_op jit(solution)/shard_map/ppermute | solution.py:37
  227.5 0.9 add.48
  228.4 2.5 collective-permute-start.2
  230.9 197.9 %collective-permute-done.2 = f32[9000,128]{1,0:T(8,128)S(1)} collective-permute-done((f32[9000,128]{1,0:T(8,128)S(1)}, f32[9000,128]{1,0:T(8,128)S(1)}, u32[]{:S(2)}, u32[]{:S(2)}) %collective-permute-start.2) | collective-permute-done | bytes 4608032 | tf_op jit(solution)/shard_map/ppermute | solution.py:37
  428.8 2.1 copy-done.3
  430.8 8.7 fusion.8
  439.5 0.4 all-reduce.11.cloned.1.call-start
  440.0 41.5 %all-reduce.9.cloned.1.call-done = f32[128,128]{0,1:T(8,128)} async-done(((f32[128,128]{0,1:T(8,128)}), f32[128,128]{0,1:T(8,128)}) %all-reduce.9.cloned.1.call-update) | async-done | bytes 65552 | tf_op jit(solution)/shard_map/psum | solution.py:42
  481.5 0.9 copy.6
  482.4 0.9 fusion.22
  483.3 11.7 %cholesky.44 = f32[128,128]{1,0:T(8,128)S(1)} custom-call(f32[128,128]{1,0:T(8,128)S(1)} %fusion.22), custom_call_target="Cholesky" | custom-call | tf_op jit(solution)/shard_map/jit(cholesky)/cholesky | solution.py:43
  495.0 0.6 compare_reduce_fusion.1
  495.7 0.7 fusion.17
  496.4 9.8 custom-call.6
  506.2 7.0 fusion.2
  513.1 24.9 %convolution_bitcast_fusion.2 = f32[1024,128]{0,1:T(8,128)} fusion(f32[128,9000]{1,0:T(8,128)S(1)} %fusion.2, f32[9000,1024]{1,0:T(8,128)} %param.6), kind=kOutput, calls=%fused_computation.12 | convolution fusion | flops 14155776000 | bytes 41996288 | tf_op jit(solution)/shard_map/dot_general | solution.py:10
  538.3 45.3 %all-reduce.11.cloned.1.call-done = f32[1024,128]{0,1:T(8,128)} async-done(((f32[1024,128]{0,1:T(8,128)}), f32[1024,128]{0,1:T(8,128)}) %all-reduce.11.cloned.1.call-update) | async-done | bytes 524304 | tf_op jit(solution)/shard_map/psum | solution.py:24
  583.6 34.4 %convolution_bitcast_fusion = f32[9000,128]{1,0:T(8,128)S(1)} fusion(f32[9000,1024]{1,0:T(8,128)} %param.6, f32[1024,128]{0,1:T(8,128)} %all-reduce.11.cloned.1.call-done, f32[1024]{0:T(1024)S(1)} %add_divide_fusion), kind=kOutput, calls=%fused_computation | convolution fusion | flops 14155907072 | bytes 42000384 | tf_op jit(solution)/shard_map/dot_general | solution.py:31
  618.1 7.7 collective-permute-done.3
  625.8 0.5 add.50
  626.3 1.6 collective-permute-start.4
  627.9 100.0 %collective-permute-done.4 = f32[9000,128]{1,0:T(8,128)S(1)} collective-permute-done((f32[9000,128]{1,0:T(8,128)S(1)}, f32[9000,128]{1,0:T(8,128)S(1)}, u32[]{:S(2)}, u32[]{:S(2)}) %collective-permute-start.4) | collective-permute-done | bytes 4608032 | tf_op jit(solution)/shard_map/ppermute | solution.py:37
  727.9 0.9 add.51
  728.8 2.5 collective-permute-start.5
  731.3 197.9 %collective-permute-done.5 = f32[9000,128]{1,0:T(8,128)S(1)} collective-permute-done((f32[9000,128]{1,0:T(8,128)S(1)}, f32[9000,128]{1,0:T(8,128)S(1)}, u32[]{:S(2)}, u32[]{:S(2)}) %collective-permute-start.5) | collective-permute-done | bytes 4608032 | tf_op jit(solution)/shard_map/ppermute | solution.py:37
  929.1 2.1 copy-done.4
  931.2 8.7 fusion.5
  939.9 0.3 all-reduce.15.cloned.1.call-start
  940.2 41.7 %all-reduce.13.cloned.1.call-done = f32[128,128]{0,1:T(8,128)} async-done(((f32[128,128]{0,1:T(8,128)}), f32[128,128]{0,1:T(8,128)}) %all-reduce.13.cloned.1.call-update) | async-done | bytes 65552 | tf_op jit(solution)/shard_map/psum | solution.py:42
  981.9 0.9 copy.8
  982.8 0.9 fusion.20
  983.7 11.7 %cholesky.55 = f32[128,128]{1,0:T(8,128)S(1)} custom-call(f32[128,128]{1,0:T(8,128)S(1)} %fusion.20), custom_call_target="Cholesky" | custom-call | tf_op jit(solution)/shard_map/jit(cholesky)/cholesky | solution.py:43
  995.4 0.6 compare_reduce_fusion
  996.1 0.7 fusion.18
  996.7 9.8 custom-call.7
  1006.5 10.2 fusion
  1016.8 2.1 copy-done.2
  1018.9 25.4 %convolution_bitcast_fusion.3 = f32[1024,128]{0,1:T(8,128)} fusion(f32[128,9000]{0,1:T(8,128)S(1)} %fusion, f32[9000,1024]{1,0:T(8,128)} %param.6), kind=kOutput, calls=%fused_computation.13 | convolution fusion | flops 14155776000 | bytes 41996288 | tf_op jit(solution)/shard_map/dot_general | solution.py:10
  1044.4 45.5 %all-reduce.15.cloned.1.call-done = f32[1024,128]{0,1:T(8,128)} async-done(((f32[1024,128]{0,1:T(8,128)}), f32[1024,128]{0,1:T(8,128)}) %all-reduce.15.cloned.1.call-update) | async-done | bytes 524304 | tf_op jit(solution)/shard_map/psum | solution.py:24
  1089.8 2.4 fusion.10
  1092.3 55.0 %all-reduce.17.cloned.1.call-done = f32[128,128]{1,0:T(8,128)} async-done(((f32[128,128]{1,0:T(8,128)}), f32[128,128]{1,0:T(8,128)}) %all-reduce.17.cloned.1.call-update) | async-done | bytes 65552 | tf_op jit(solution)/shard_map/psum | solution.py:52
  1147.3 1.5 copy.17
  (24 shorter events, 0.7 us)
Async XLA Ops:
  7.2 27.8 %copy-start.5 = (f32[1024]{0:T(1024)S(1)}, f32[1024]{0:T(1024)}, u32[]{:S(2)}) copy-start(f32[1024]{0:T(1024)} %param.7) | copy-start | bytes 12292
  7.2 76.0 %all-reduce.7.cloned.1.call-start = ((), (), s32[]{:S(2)}) async-start(), calls=%async_computation | async-start | bytes 1048576 | tf_op jit(solution)/shard_map/psum | solution.py:24
  34.9 446.6 %all-reduce.9.cloned.1.call-start = ((), (), s32[]{:S(2)}) async-start(), calls=%async_computation.1 | async-start | bytes 131072 | tf_op jit(solution)/shard_map/psum | solution.py:42
  117.6 7.8 collective-permute-start
  126.0 101.5 %collective-permute-start.1 = (f32[9000,128]{1,0:T(8,128)S(1)}, f32[9000,128]{1,0:T(8,128)S(1)}, u32[]{:S(2)}, u32[]{:S(2)}) collective-permute-start(f32[9000,128]{1,0:T(8,128)S(1)} %add.47), channel_id=1, source_target_pairs={{0,8},{4,12},{8,0},{12,4},{16,24},{20,28},{24,16},{28,20},{1,9},{5... | collective-permute-start | bytes 13824008 | tf_op jit(solution)/shard_map/ppermute | solution.py:37
  228.4 200.4 %copy-start = (f32[9000,128]{1,0:T(8,128)}, f32[9000,128]{1,0:T(8,128)S(1)}, u32[]{:S(2)}) copy-start(f32[9000,128]{1,0:T(8,128)S(1)} %add.48) | copy-start | bytes 13824004
  228.4 200.3 %collective-permute-start.2 = (f32[9000,128]{1,0:T(8,128)S(1)}, f32[9000,128]{1,0:T(8,128)S(1)}, u32[]{:S(2)}, u32[]{:S(2)}) collective-permute-start(f32[9000,128]{1,0:T(8,128)S(1)} %add.48), channel_id=1, source_target_pairs={{0,16},{4,20},{8,24},{12,28},{16,0},{20,4},{24,8},{28,12},{1,17},{... | collective-permute-start | bytes 13824008 | tf_op jit(solution)/shard_map/ppermute | solution.py:37
  428.8 2.1 copy-start.3
  439.5 144.1 %all-reduce.11.cloned.1.call-start = ((), (), s32[]{:S(2)}) async-start(), calls=%async_computation.2 | async-start | bytes 1048576 | tf_op jit(solution)/shard_map/psum | solution.py:24
  538.0 443.8 %all-reduce.13.cloned.1.call-start = ((), (), s32[]{:S(2)}) async-start(), calls=%async_computation.3 | async-start | bytes 131072 | tf_op jit(solution)/shard_map/psum | solution.py:42
  618.0 7.8 collective-permute-start.3
  626.3 101.5 %collective-permute-start.4 = (f32[9000,128]{1,0:T(8,128)S(1)}, f32[9000,128]{1,0:T(8,128)S(1)}, u32[]{:S(2)}, u32[]{:S(2)}) collective-permute-start(f32[9000,128]{1,0:T(8,128)S(1)} %add.50), channel_id=1, source_target_pairs={{0,8},{4,12},{8,0},{12,4},{16,24},{20,28},{24,16},{28,20},{1,9},{5... | collective-permute-start | bytes 13824008 | tf_op jit(solution)/shard_map/ppermute | solution.py:37
  728.8 200.4 %copy-start.1 = (f32[9000,128]{1,0:T(8,128)}, f32[9000,128]{1,0:T(8,128)S(1)}, u32[]{:S(2)}) copy-start(f32[9000,128]{1,0:T(8,128)S(1)} %add.51) | copy-start | bytes 13824004
  728.8 200.3 %collective-permute-start.5 = (f32[9000,128]{1,0:T(8,128)S(1)}, f32[9000,128]{1,0:T(8,128)S(1)}, u32[]{:S(2)}, u32[]{:S(2)}) collective-permute-start(f32[9000,128]{1,0:T(8,128)S(1)} %add.51), channel_id=1, source_target_pairs={{0,16},{4,20},{8,24},{12,28},{16,0},{20,4},{24,8},{28,12},{1,17},{... | collective-permute-start | bytes 13824008 | tf_op jit(solution)/shard_map/ppermute | solution.py:37
  929.1 2.1 copy-start.4
  939.9 149.9 %all-reduce.15.cloned.1.call-start = ((), (), s32[]{:S(2)}) async-start(), calls=%async_computation.4 | async-start | bytes 1048576 | tf_op jit(solution)/shard_map/psum | solution.py:24
  1016.7 2.2 copy-start.2
  1044.3 103.0 %all-reduce.17.cloned.1.call-start = ((), (), s32[]{:S(2)}) async-start(), calls=%async_computation.5 | async-start | bytes 131072 | tf_op jit(solution)/shard_map/psum | solution.py:52
Sparse Core Ops, SparseCore 0:
  35.1 48.0 all-reduce.6
  439.6 41.8 all-reduce.8
  538.2 45.3 all-reduce.10
  940.0 41.8 all-reduce.12
  1044.5 45.3 all-reduce.14
  1092.6 54.6 all-reduce.16
